TPU v7x, 512 devices: a whole 4x8x8 slice. The times are simulated.
512 devices in a mesh: seed: 2 (over core), dp: 4 (over x), tensor: 64 (over z, y).
Axes of the slice: x: 4, y: 8, z: 8, core: 2. Of those that a mesh axis runs over, the one named last changes fastest.
Arguments:
- hidden: bfloat16 [2, 64, 96, 2048], P('seed', 'dp', None, 'tensor'), may hold values from -24 to 24
- norm_gain: float32 [2, 2048], P('seed'), may hold values from 0.25 to 1.75
- lm_head: bfloat16 [2, 2048, 65536], P('seed', None, 'tensor'), may hold values from -3 to 3
- targets: int32 [64, 96], P('dp'), may hold values from 0 to 65535
- lengths: int32 [64], P('dp'), may hold values from 24 to 96
Outputs:
- token_scores: float32 [2, 64, 96], P('seed', 'dp')
- ensemble: float32 [64], P('dp')
- centered: float32 [64], P('dp')
All inputs are finite; a program needn't handle non-finite values.
Results may differ from a plain program's by a relative error of at most 0.0003.
The roundings to bfloat16 on the way count: a program that leaves them out, or rounds other values in their place, can miss the bound.
Values may be sent and summed in bfloat16 or wider, within the bound.
A program may use at most 128 MiB of HBM per device.

v0:
```python
import jax
import jax.numpy as jnp
from jax import lax
from jax.sharding import Mesh
from jax.sharding import PartitionSpec as P

TENSOR = ("tensor_0", "tensor_1")


rms_epsilon = 1e-05


def gathered_once(x, axis):
    leaves = jax.tree.leaves(x)
    sequence = sorted(range(len(leaves)), key=lambda k: -leaves[k].size)
    width = (1, *leaves[sequence[0]].shape)[-1]
    lines = [
        jnp.pad(leaves[k].reshape(-1), (0, -leaves[k].size % width)).reshape(-1, width)
        for k in sequence
    ]
    both, at, found = (lax.all_gather(jnp.concatenate(lines), axis), 0, {})
    for k, line in zip(sequence, lines):
        piece = both[:, at : at + len(line)].reshape(len(both), -1)
        found[k] = piece[:, : leaves[k].size].reshape(-1, *leaves[k].shape)
        at += len(line)
    numbers = iter(range(len(leaves)))
    return jax.tree.map(lambda _: found[next(numbers)], x)


def joined_all(x, axes, combine):
    for axis in axes:
        pieces = gathered_once(x, axis)
        x = jax.tree.map(lambda part: part[0], pieces)
        for k in range(1, lax.axis_size(axis)):
            x = combine(x, jax.tree.map(lambda part: part[k], pieces))
    return x


def from_everyone(x, axis):
    peers = lax.axis_size(axis)
    return lax.all_to_all(jnp.broadcast_to(x[None], (peers, *x.shape)), axis, 0, 0, tiled=True)


def taken_together(x, axis):
    return from_everyone(x, axis).sum(axis=0)


def combine_parts(first, second):
    top_value = jnp.maximum(first[0], second[0])
    left = jnp.exp(first[0] - top_value)
    right = jnp.exp(second[0] - top_value)
    return (
        top_value,
        first[1] * left + second[1] * right,
        first[2] * left * left + second[2] * right * right,
        first[3] * left + second[3] * right,
    )


def shards(hidden, norm_gain, lm_head, targets, lengths):
    per_group, seq_len, own_width = (hidden.shape[1], hidden.shape[2], hidden.shape[3])
    full_width = norm_gain.shape[1]
    own_vocab = lm_head.shape[2]
    row_count = per_group * seq_len
    weight = lm_head[0]
    gain = norm_gain[0]
    whole = lax.all_gather(hidden, TENSOR, axis=3, tiled=True)
    flat = whole.reshape(row_count, full_width).astype(jnp.float32)
    mean_sq = jnp.mean(flat * flat, axis=1, keepdims=True)
    normed = (flat * lax.rsqrt(mean_sq + rms_epsilon) * gain).astype(jnp.bfloat16)
    logits = jnp.dot(normed, weight, preferred_element_type=jnp.float32)
    first_column = lax.axis_index(TENSOR) * own_vocab
    column = jnp.arange(own_vocab, dtype=jnp.int32) + first_column
    onehot = column[None, :] == targets.reshape(row_count)[:, None]
    local_top = jnp.max(logits, axis=1)
    scaled_exp = jnp.exp(logits - local_top[:, None])
    merged = joined_all(
        (
            local_top,
            jnp.sum(scaled_exp, axis=1),
            jnp.sum(scaled_exp * scaled_exp, axis=1),
            jnp.sum(jnp.where(onehot, scaled_exp, 0.0), axis=1),
        ),
        TENSOR,
        combine_parts,
    )
    exp_mass, exp_square, exp_target = (merged[1], merged[2], merged[3])
    spread = jnp.maximum(
        exp_square / (exp_mass * exp_mass) - 2.0 * exp_target / exp_mass + 1.0, 0.0
    )
    scores = jnp.sqrt(spread).reshape(per_group, seq_len)
    position = jnp.arange(seq_len, dtype=jnp.int32)
    valid = position[None, :] < lengths[:, None]
    token_scores = jnp.where(valid, scores, jnp.float32(0.0))
    example_scores = jnp.sum(token_scores, axis=1) / lengths.astype(jnp.float32)
    members = lax.axis_size("seed")
    groups = lax.axis_size("dp")
    slots = jnp.zeros((groups * per_group,), jnp.float32)
    slots = lax.dynamic_update_slice_in_dim(
        slots, example_scores, lax.axis_index("dp") * per_group, 0
    )
    everyone = taken_together(slots, ("seed", "dp")) / members
    ensemble = lax.dynamic_slice_in_dim(everyone, lax.axis_index("dp") * per_group, per_group, 0)
    centered = ensemble - jnp.sum(everyone) / (per_group * groups)
    return (token_scores[None, :, :], ensemble, centered)


def solution(mesh):
    finer = Mesh(
        mesh.devices.reshape(mesh.shape["seed"], mesh.shape["dp"], 8, 8),
        ("seed", "dp", "tensor_0", "tensor_1"),
    )
    in_specs = (
        P("seed", "dp", None, TENSOR),
        P("seed", None),
        P("seed", None, TENSOR),
        P("dp", None),
        P("dp"),
    )
    out_specs = (P("seed", "dp", None), P("dp"), P("dp"))
    return jax.shard_map(
        shards, mesh=finer, in_specs=in_specs, out_specs=out_specs, check_vma=False
    )
```

profile of v0, /device:TPU:1, one launch (start us, length us, event | category | flops | bytes accessed | tf_op | source)
XLA Modules:
  0.0 219.5 jit_solution(6617547372947440160)
XLA Ops:
  7.2 1.6 copy.13
  8.9 0.8 eq.16
  9.6 105.8 %all-gather.6.cloned.1.call-done = bf16[1,16,96,2048]{2,1,0,3:T(8,128)(2,1)} async-done(((bf16[1,16,96,32]{2,1,0,3:T(8,128)(2,1)}), bf16[1,16,96,2048]{2,1,0,3:T(8,128)(2,1)}) %all-gather.6.cloned.1.call-update) | async-done | bytes 6291472 | tf_op jit(solution)/shard_map/all_gather | solution.py:67
  115.4 11.8 %copy.14 = bf16[1,16,96,2048]{3,2,1,0:T(8,128)(2,1)} copy(bf16[1,16,96,2048]{2,1,0,3:T(8,128)(2,1)} %all-gather.6.cloned.1.call-done) | data formatting | bytes 12582912 | tf_op jit(solution)/shard_map/all_gather | solution.py:67
  127.2 4.2 %fusion = f32[16,96]{1,0:T(8,128)S(1)} fusion(bf16[1,16,96,2048]{3,2,1,0:T(8,128)(2,1)} %copy.14), kind=kLoop, calls=%fused_computation.2 | loop fusion | flops 9435648 | bytes 6297600 | tf_op jit(solution)/shard_map/reduce_sum | solution.py:69
  131.4 0.3 copy-done
  131.8 1.5 fusion.2
  133.3 0.7 copy-done.3
  134.0 7.4 %fusion.103 = (f32[1536]{0:T(1024)S(1)}, f32[1536,1024]{0,1:T(8,128)S(1)}) fusion(bf16[1536,2048]{1,0:T(8,128)(2,1)S(1)} %bitcast.341, bf16[1,2048,1024]{2,1,0:T(8,128)(2,1)S(1)} %copy-done.3), kind=kOutput, calls=%fused_computation.251 | convolution fusion | flops 6444022272 | bytes 16783360 | tf_op jit(solution)/shard_map/dot_general | solution.py:71
  141.4 2.3 %fusion.3 = (f32[1536]{0:T(1024)S(1)}, f32[1536]{0:T(1024)S(1)}, f32[1536]{0:T(1024)S(1)}) fusion(f32[1536,1024]{0,1:T(8,128)S(1)} %get-tuple-element.48, f32[1536]{0:T(1024)S(1)} %get-tuple-element.47, s32[1536]{0:T(1024)S(1)} %eq.16, s32[1024]{0:T(1024)S(1)} %iota_add_fusion), kind=kLoop, calls=%fused_computation.8 | loop fusion | flops 11005440 | bytes 6326272 | tf_op jit(solution)/shard_map/reduce_sum | solution.py:80
  143.8 19.5 %all-gather.2 = f32[8,4,1536]{2,1,0:T(4,128)S(1)} all-gather(f32[1,4,1536]{2,1,0:T(4,128)S(1)} %maximum_bitcast_fusion), channel_id=2, replica_groups=mesh['seed'=2,'dp'=4,'tensor_0'=8,'tensor_1'=8] {'tensor_0'}, dimensions={0}, use_global_device_ids=true | all-gather | bytes 221184 | tf_op jit(solution)/shard_map/all_gather | solution.py:21
  163.4 0.1 fusion.71
  163.5 0.2 fusion.48
  163.7 0.1 fusion.50
  163.9 18.9 %all-gather.3 = f32[8,4,1536]{2,1,0:T(4,128)S(1)} all-gather(f32[1,4,1536]{2,1,0:T(4,128)S(1)} %maximum_bitcast_fusion.1), channel_id=3, replica_groups=mesh['seed'=2,'dp'=4,'tensor_0'=8,'tensor_1'=8] {'tensor_1'}, dimensions={0}, use_global_device_ids=true | all-gather | bytes 221184 | tf_op jit(solution)/shard_map/all_gather | solution.py:21
  182.7 0.3 slice_reduce_fusion.30
  183.0 0.2 slice_reduce_fusion.31
  183.3 0.1 squeeze.325
  186.1 0.1 squeeze.326
  186.2 0.1 squeeze.294
  186.3 0.1 squeeze.327
  186.3 0.1 squeeze.295
  186.4 0.1 squeeze.328
  186.5 0.1 squeeze.296
  186.6 0.1 squeeze.329
  186.6 0.1 squeeze.297
  186.7 0.1 squeeze.330
  186.8 0.1 squeeze.298
  186.8 0.1 squeeze.331
  186.9 0.1 squeeze.299
  187.1 0.1 squeeze.300
  187.1 0.1 squeeze.333
  187.2 0.1 squeeze.301
  187.3 0.1 squeeze.334
  187.4 0.1 squeeze.302
  187.4 0.1 squeeze.335
  187.5 0.1 squeeze.303
  187.6 0.1 squeeze.336
  187.7 0.1 squeeze.304
  187.7 0.1 squeeze.355
  187.9 0.2 select_reduce_fusion.1
  188.1 0.1 divide_dynamic-update-slice_fusion
  188.2 0.6 broadcast_in_dim.8
  188.8 17.4 %all-to-all-start = ((f32[8,1,64]{2,1,0:T(1,128)}), f32[8,1,64]{2,1,0:T(1,128)S(1)}, u32[]{:S(2)}, u32[]{:S(2)}) async-start(f32[8,1,64]{2,1,0:T(1,128)} %broadcast_in_dim.8), calls=%async_computation | async-start | bytes 8192 | tf_op jit(solution)/shard_map/all_to_all | solution.py:41
  206.2 0.7 sqrt_select_fusion
  206.9 3.9 %all-to-all-done = f32[8,1,64]{2,1,0:T(1,128)S(1)} async-done(((f32[8,1,64]{2,1,0:T(1,128)}), f32[8,1,64]{2,1,0:T(1,128)S(1)}, u32[]{:S(2)}, u32[]{:S(2)}) %all-to-all-start) | async-done | bytes 2080 | tf_op jit(solution)/shard_map/all_to_all | solution.py:41
  210.8 0.6 broadcast_multiply_fusion
  212.1 0.6 broadcast_subtract_fusion
  (59 shorter events, 3.1 us)
Async XLA Ops:
  7.2 108.2 %all-gather.6.cloned.1.call-start = ((), (), s32[]{:S(2)}) async-start(), calls=%async_computation.1 | async-start | bytes 8519680 | tf_op jit(solution)/shard_map/all_gather | solution.py:67
  127.2 4.6 %copy-start = (bf16[1,16,96,2048]{3,2,1,0:T(8,128)(2,1)S(1)}, bf16[1,16,96,2048]{3,2,1,0:T(8,128)(2,1)}, u32[]{:S(2)}) copy-start(bf16[1,16,96,2048]{3,2,1,0:T(8,128)(2,1)} %copy.14) | copy-start | bytes 18874372
  127.2 4.6 %copy-start.1 = (f32[1,2048]{1,0:T(1,128)S(1)}, f32[1,2048]{1,0:T(1,128)}, u32[]{:S(2)}) copy-start(f32[1,2048]{1,0:T(1,128)} %param.6) | copy-start | bytes 24580
  131.8 2.2 copy-start.3
  141.4 46.5 %copy-start.2 = (s32[16]{0:T(128)S(1)}, s32[16]{0:T(128)}, u32[]{:S(2)}) copy-start(s32[16]{0:T(128)} %param.9) | copy-start | bytes 196
  188.8 22.0 %all-to-all-start = ((f32[8,1,64]{2,1,0:T(1,128)}), f32[8,1,64]{2,1,0:T(1,128)S(1)}, u32[]{:S(2)}, u32[]{:S(2)}) async-start(f32[8,1,64]{2,1,0:T(1,128)} %broadcast_in_dim.8), calls=%async_computation | async-start | bytes 8192 | tf_op jit(solution)/shard_map/all_to_all | solution.py:41
Sparse Core Ops, SparseCore 0:
  11.0 104.3 all-gather.5
where the time goes:
time: 220 us
  waiting for transfers between devices  110 us (50%)
  blocking collectives  38.4 us (17%)
  local copies, waits for them, and re-layouts  20.9 us (10%)
  starting transfers between devices  17.4 us (8%)
  between operations  14.9 us (7%)
  other arithmetic  10.9 us (5%)
  matrix products  7.38 us (3%)
    all_gather x1, waiting for transfers between devices, shards(): whole = lax.all_gather(hidden, TENSOR, axis=3, tiled=True)  106 us
    all_gather x2, blocking collectives, gathered_once(): both, at, found = (lax.all_gather(jnp.concatenate(lines), axis), 0, {})  38.4 us
    all_to_all x1, starting transfers between devices, from_everyone(): lax.all_to_all(jnp.broadcast_to(x[None], (peers, *x.shape)), axis, 0, 0,...  17.4 us
    all_gather x1, local copies, waits for them, and re-layouts, shards(): whole = lax.all_gather(hidden, TENSOR, axis=3, tiled=True)  11.8 us
    dot_general x1, matrix products, shards(): logits = jnp.dot(normed, weight, preferred_element_type=jnp.float32)  7.38 us
  transfers between devices with their start and end apart: 2, of which 2 were waited for; matrix products, arithmetic and copies ran while one was open for 1% of the time, Pallas kernels for 0%

commit v1 on v0

v1 whole, which is shorter than its diff:
```python
import functools

import jax
import jax.numpy as jnp
from jax import lax
from jax.experimental import pallas as pl
from jax.experimental.pallas import tpu as pltpu
from jax.sharding import Mesh
from jax.sharding import PartitionSpec as P

MESH = pl.DeviceIdType.MESH
TENSOR = ("tensor_0", "tensor_1")
LANES = 128
RMS_EPSILON = 1e-05


def kernel(
    sizes,
    hidden_hbm,
    gain_hbm,
    weight_hbm,
    target_hbm,
    length_ref,
    token_ref,
    ensemble_ref,
    centered_ref,
    gathered,
    hidden_own,
    gain_own,
    weight_own,
    target_own,
    weight_turned,
    gain_wide,
    target_lanes,
    logits,
    normed,
    stats_y,
    stats_z,
    scores,
    examples,
    load_sem,
    send_sem,
    recv_sem,
    stat_send,
    stat_recv,
    end_send,
    end_recv,
):
    ring, members, groups, batch, seq, width = sizes
    half_ring = ring // 2
    chunks = gathered.shape[0]
    units = chunks // 2
    depth = gathered.shape[1] * gathered.shape[2] * width
    vocab = weight_own.shape[1]
    s, d = lax.axis_index("seed"), lax.axis_index("dp")
    z, y = lax.axis_index("tensor_0"), lax.axis_index("tensor_1")

    def along_z(k):
        return lax.rem(z + (k + ring), ring)

    def along_y(k):
        return lax.rem(y + (k + ring), ring)

    barrier = pltpu.get_barrier_semaphore()
    others = [(a, b) for a in range(members) for b in range(groups) if a or b]
    for k in range(1, ring):
        pl.semaphore_signal(barrier, inc=1, device_id={"tensor_0": along_z(k)}, device_id_type=MESH)
        pl.semaphore_signal(barrier, inc=1, device_id={"tensor_1": along_y(k)}, device_id_type=MESH)
    for a, b in others:
        pl.semaphore_signal(
            barrier,
            inc=1,
            device_id={"seed": lax.rem(s + a, members), "dp": lax.rem(d + b, groups)},
            device_id_type=MESH,
        )
    loads = [
        pltpu.make_async_copy(hidden_hbm, hidden_own, load_sem.at[0]),
        pltpu.make_async_copy(target_hbm, target_own, load_sem.at[1]),
        pltpu.make_async_copy(gain_hbm, gain_own, load_sem.at[2]),
        pltpu.make_async_copy(weight_hbm, weight_own, load_sem.at[3]),
    ]
    for load in loads:
        load.start()

    loads[0].wait()
    for q in range(batch // 4):
        part = [hidden_own[4 * q + r].astype(jnp.float32) for r in range(4)]
        joined = lanes_joined(part)
        for r in range(3):
            gathered[3 * q + r, z, y] = joined[r].astype(jnp.bfloat16)
    pl.semaphore_wait(barrier, 2 * (ring - 1) + len(others))

    pending = []
    count = [0]

    def message(view, at, axis, sign):
        number = count[0]
        count[0] += 1
        step = (sign, 0) if axis == 0 else (0, sign)
        device = {"tensor_0": along_z(sign)} if axis == 0 else {"tensor_1": along_y(sign)}

        def copy(place):
            return pltpu.make_async_remote_copy(
                src_ref=view(*place),
                dst_ref=view(*place),
                send_sem=send_sem.at[number],
                recv_sem=recv_sem.at[number],
                device_id=device,
                device_id_type=MESH,
            )

        sent = copy(at)
        sent.start()
        pending.append(sent)
        return copy((at[0] - step[0], at[1] - step[1])), (at[0] - step[0], at[1] - step[1])

    def shard_view(kind, first, number):
        def view(dz, dy):
            return gathered.at[pl.ds(kind * units + first, number), along_z(dz), along_y(dy)]

        return view

    def block_view(kind, unit, part):
        def view(dz, dy):
            if kind == 0:
                return gathered.at[unit, along_z(dz), pl.ds(*part)]
            return gathered.at[units + unit, pl.ds(*part), along_y(dy)]

        return view

    first_axis = {0: 1, 1: 0}
    whole = (0, units)
    halves = {1: (0, units // 2), -1: (units // 2, units - units // 2)}
    phase_one = {}
    arriving = []
    for kind in (0, 1):
        for sign in (1, -1):
            phase_one[kind, sign] = message(shard_view(kind, *whole), (0, 0), first_axis[kind], sign)
    for kind in (0, 1):
        for sign in (1, -1):
            arriving.append(message(shard_view(kind, *whole), (0, 0), 1 - first_axis[kind], sign)[0])

    prepared = [0]

    def prepare(upto):
        while prepared[0] < min(upto, depth // 256):
            k = prepared[0]
            if k == 0:
                loads[1].wait()
                loads[2].wait()
                loads[3].wait()
                for q in range(batch // 4):
                    part = [target_own[pl.ds(4 * q + r, 1), :] for r in range(4)]
                    joined = lanes_joined(part)
                    for r in range(3):
                        target_lanes[pl.ds(3 * q + r, 1), :] = joined[r]
                for b in range(depth // LANES):
                    row = gain_own[:, b * LANES : (b + 1) * LANES]
                    gain_wide[b * LANES : (b + 1) * LANES, :] = jnp.broadcast_to(
                        row, (LANES, LANES)
                    ).T
            for v in range(vocab // 256):
                block = weight_own[k * 256 : (k + 1) * 256, v * 256 : (v + 1) * 256]
                weight_turned[v * 256 : (v + 1) * 256, k * 256 : (k + 1) * 256] = block.T
            prepared[0] += 1

    for step in range(1, half_ring + 1):
        prepare(step * depth // 256 // half_ring)
        places = {}
        for kind in (0, 1):
            for sign in (1, -1):
                copy, at = phase_one[kind, sign]
                copy.wait_recv()
                places[kind, sign] = at
                if step < half_ring:
                    span = whole if step + 1 < half_ring else halves[sign]
                    phase_one[kind, sign] = message(
                        shard_view(kind, *span), at, first_axis[kind], sign
                    )
        for kind in (0, 1):
            for sign in (1, -1) if step < half_ring else (1,):
                for way in (1, -1):
                    arriving.append(
                        message(
                            shard_view(kind, *whole), places[kind, sign], 1 - first_axis[kind], way
                        )[0]
                    )
    for copy in arriving:
        copy.wait_recv()

    def unit_stats(u):
        for side, c in enumerate((u, units + u)):
            total = jnp.zeros((1, LANES), jnp.float32)
            for b in range(depth // 256):
                x = gathered[c, b].reshape(256, LANES).astype(jnp.float32)
                total += jnp.sum(x * x, axis=0, keepdims=True)
            scale = lax.rsqrt(total * (1.0 / depth) + RMS_EPSILON)
            for b in range(depth // 256):
                x = gathered[c, b].reshape(256, LANES).astype(jnp.float32)
                gain = gain_wide[b * 256 : (b + 1) * 256, :]
                normed[b * 256 : (b + 1) * 256, side * LANES : (side + 1) * LANES] = (
                    x * scale * gain
                ).astype(jnp.bfloat16)
        for v in range(vocab // 256):
            logits[v * 256 : (v + 1) * 256, :] = jnp.dot(
                weight_turned[v * 256 : (v + 1) * 256, :],
                normed[...],
                preferred_element_type=jnp.float32,
            )
        own_first = (z * ring + y) * vocab
        rows = []
        for side, c in enumerate((u, units + u)):
            block = logits[:, side * LANES : (side + 1) * LANES]
            top = jnp.max(block, axis=0, keepdims=True)
            wanted = target_lanes[pl.ds(c, 1), :] - own_first
            column = lax.broadcasted_iota(jnp.int32, (vocab, LANES), 0)
            scaled = jnp.exp(block - top)
            hit = column == wanted
            other = jnp.where(hit, 0.0, scaled)
            rows.append(
                (
                    top,
                    jnp.sum(other, axis=0, keepdims=True),
                    jnp.sum(other * other, axis=0, keepdims=True),
                    jnp.sum(jnp.where(hit, scaled, 0.0), axis=0, keepdims=True),
                )
            )
        return jnp.concatenate([rows[side][k] for k in range(4) for side in range(2)], axis=0)

    def stat_copy(buffer, u, level, k):
        if level == 0:
            device, mine = {"tensor_1": along_y(k)}, y
        else:
            device, mine = {"tensor_0": along_z(k)}, z

        def copy(place):
            return pltpu.make_async_remote_copy(
                src_ref=buffer.at[u, place],
                dst_ref=buffer.at[u, place],
                send_sem=stat_send.at[u, level, k],
                recv_sem=stat_recv.at[u, level, k],
                device_id=device,
                device_id_type=MESH,
            )

        back = lax.rem(mine + (ring - k), ring)
        return copy(mine), copy(back)

    arrivals = {}

    def share(buffer, u, level, value):
        buffer[u, y if level == 0 else z] = value
        arrivals[u, level] = []
        for k in sorted(range(1, ring), key=lambda k: -min(k, ring - k)):
            sent, back = stat_copy(buffer, u, level, k)
            sent.start()
            pending.append(sent)
            arrivals[u, level].append(back)

    def combined(buffer, u, level):
        for copy in arrivals[u, level]:
            copy.wait_recv()
        parts = buffer[u]
        tops = parts[:, 0:2]
        top = jnp.max(tops, axis=0)
        scale = jnp.exp(tops - top[None])
        return jnp.concatenate(
            [
                top,
                jnp.sum(parts[:, 2:4] * scale, axis=0),
                jnp.sum(parts[:, 4:6] * scale * scale, axis=0),
                jnp.sum(parts[:, 6:8] * scale, axis=0),
            ],
            axis=0,
        )

    def finish(u):
        value = combined(stats_z, u, 1)
        other, square, wanted = (value[2:4], value[4:6], value[6:8])
        score = jnp.sqrt(other * other + square) / (other + wanted)
        scores[pl.ds(u, 1), :] = score[0:1]
        scores[pl.ds(units + u, 1), :] = score[1:2]

    hops = {}
    last = half_ring - 1
    for slot in range(units + last + 2):
        for hop in range(2, half_ring + 1):
            unit = slot - (hop - 2)
            if not 0 <= unit < units:
                continue
            for kind in (0, 1):
                for sign in (1, -1):
                    if hop == 2:
                        at = (-sign, 0) if kind == 0 else (0, -sign)
                    else:
                        copy, at = hops[kind, sign, unit]
                        copy.wait_recv()
                    part = (0, ring)
                    if hop == half_ring:
                        part = (0, half_ring) if sign == 1 else (half_ring, ring - half_ring)
                    hops[kind, sign, unit] = message(
                        block_view(kind, unit, part), at, 1 - first_axis[kind], sign
                    )
        unit = slot - last
        if 0 <= unit < units:
            for kind in (0, 1):
                for sign in (1, -1):
                    hops[kind, sign, unit][0].wait_recv()
            share(stats_y, unit, 0, unit_stats(unit))
        if 0 <= unit - 1 < units:
            share(stats_z, unit - 1, 1, combined(stats_y, unit - 1, 0))
        if 0 <= unit - 2 < units:
            finish(unit - 2)

    for q in range(batch // 4):
        part = [scores[pl.ds(3 * q + r, 1), :] for r in range(3)]
        split = [
            part[0][:, :seq],
            jnp.concatenate([part[0][:, 96:], part[1][:, :64]], axis=1),
            jnp.concatenate([part[1][:, 64:], part[2][:, :32]], axis=1),
            part[2][:, 32:],
        ]
        for r in range(4):
            token_ref[pl.ds(4 * q + r, 1), :] = split[r]
    example = lax.broadcasted_iota(jnp.int32, (batch, seq), 0)
    length = jnp.zeros((batch, seq), jnp.int32)
    for b in range(batch):
        length = jnp.where(example == b, length_ref[b], length)
    position = lax.broadcasted_iota(jnp.int32, (batch, seq), 1)
    token = jnp.where(position < length, token_ref[...], 0.0)
    token_ref[...] = token
    mean = jnp.sum(token, axis=1, keepdims=True) / length.astype(jnp.float32)[:, :1]
    examples[s * groups + d] = jnp.broadcast_to(mean, (batch, LANES))

    waiting = []
    for a, b in others:

        def copy(place):
            return pltpu.make_async_remote_copy(
                src_ref=examples.at[place],
                dst_ref=examples.at[place],
                send_sem=end_send.at[a, b],
                recv_sem=end_recv.at[a, b],
                device_id={"seed": lax.rem(s + a, members), "dp": lax.rem(d + b, groups)},
                device_id_type=MESH,
            )

        sent = copy(s * groups + d)
        sent.start()
        pending.append(sent)
        waiting.append(
            copy(lax.rem(s + members - a, members) * groups + lax.rem(d + groups - b, groups))
        )
    for copy in waiting:
        copy.wait_recv()
    total = jnp.zeros((batch, LANES), jnp.float32)
    own = jnp.zeros((batch, LANES), jnp.float32)
    for b in range(groups):
        pair = examples[b]
        for a in range(1, members):
            pair += examples[a * groups + b]
        pair = pair * (1.0 / members)
        total += pair
        own = jnp.where(d == b, pair, own)
    average = jnp.sum(total, axis=0, keepdims=True) * (1.0 / (groups * batch))
    row = lax.broadcasted_iota(jnp.int32, (batch, LANES), 0)
    lane = lax.broadcasted_iota(jnp.int32, (batch, LANES), 1)
    ensemble = jnp.sum(jnp.where(row == lane, own, 0.0), axis=0, keepdims=True)
    ensemble_ref[...] = ensemble[:, :batch]
    centered_ref[...] = (ensemble - average)[:, :batch]
    for copy in pending:
        copy.wait_send()


def lanes_joined(part):
    return (
        jnp.concatenate([part[0], part[1][:, :32]], axis=1),
        jnp.concatenate([part[1][:, 32:], part[2][:, :64]], axis=1),
        jnp.concatenate([part[2][:, 64:], part[3]], axis=1),
    )


def shards(ring, members, groups, hidden, norm_gain, lm_head, targets, lengths):
    batch, seq, width = hidden.shape[1:]
    depth, vocab = lm_head.shape[1:]
    chunks = batch * seq // LANES
    units = chunks // 2
    half = ring // 2
    messages = 4 * half + 4 * (2 * half) + 4 * (half - 1) * units
    far = pl.BlockSpec(memory_space=pltpu.HBM)
    vmem = pl.BlockSpec(memory_space=pltpu.VMEM)
    f32 = jnp.float32
    token, ensemble, centered = pl.pallas_call(
        functools.partial(kernel, (ring, members, groups, batch, seq, width)),
        out_shape=(
            jax.ShapeDtypeStruct((batch, seq), f32),
            jax.ShapeDtypeStruct((1, batch), f32),
            jax.ShapeDtypeStruct((1, batch), f32),
        ),
        in_specs=[far] * 4 + [pl.BlockSpec(memory_space=pltpu.SMEM)],
        out_specs=(vmem, vmem, vmem),
        scratch_shapes=[
            pltpu.VMEM((chunks, ring, ring, width, LANES), jnp.bfloat16),
            pltpu.VMEM((batch, width, seq), jnp.bfloat16),
            pltpu.VMEM((1, depth), f32),
            pltpu.VMEM((depth, vocab), jnp.bfloat16),
            pltpu.VMEM((batch, seq), jnp.int32),
            pltpu.VMEM((vocab, depth), jnp.bfloat16),
            pltpu.VMEM((depth, LANES), f32),
            pltpu.VMEM((chunks, LANES), jnp.int32),
            pltpu.VMEM((vocab, 2 * LANES), f32),
            pltpu.VMEM((depth, 2 * LANES), jnp.bfloat16),
            pltpu.VMEM((units, ring, 8, LANES), f32),
            pltpu.VMEM((units, ring, 8, LANES), f32),
            pltpu.VMEM((chunks, LANES), f32),
            pltpu.VMEM((members * groups, batch, LANES), f32),
            pltpu.SemaphoreType.DMA((4,)),
            pltpu.SemaphoreType.DMA((messages,)),
            pltpu.SemaphoreType.DMA((messages,)),
            pltpu.SemaphoreType.DMA((units, 2, ring)),
            pltpu.SemaphoreType.DMA((units, 2, ring)),
            pltpu.SemaphoreType.DMA((members, groups)),
            pltpu.SemaphoreType.DMA((members, groups)),
        ],
        compiler_params=pltpu.CompilerParams(
            collective_id=0, has_side_effects=True, vmem_limit_bytes=67043328
        ),
    )(
        hidden[0].transpose(0, 2, 1),
        norm_gain,
        lm_head[0],
        targets,
        lengths,
    )
    return token[None], ensemble[0], centered[0]


def solution(mesh):
    ring = 8
    finer = Mesh(
        mesh.devices.reshape(mesh.shape["seed"], mesh.shape["dp"], ring, ring),
        ("seed", "dp", "tensor_0", "tensor_1"),
    )
    in_specs = (
        P("seed", "dp", None, TENSOR),
        P("seed", None),
        P("seed", None, TENSOR),
        P("dp", None),
        P("dp"),
    )
    out_specs = (P("seed", "dp", None), P("dp"), P("dp"))
    return jax.shard_map(
        functools.partial(shards, ring, mesh.shape["seed"], mesh.shape["dp"]),
        mesh=finer,
        in_specs=in_specs,
        out_specs=out_specs,
        check_vma=False,
    )
```

time: 220 us -> 92.4 us (0.42)
  waiting for transfers between devices: 110 us -> 0 us
  Pallas kernels: 0 us -> 87.9 us
  blocking collectives: 38.4 us -> 0 us
  starting transfers between devices: 17.4 us -> 0 us
  local copies, waits for them, and re-layouts: 20.9 us -> 3.61 us
  between operations: 14.9 us -> 0.64 us
  other arithmetic: 10.9 us -> 0 us
  matrix products: 7.38 us -> 0 us
    all_gather x1 -> x0, waiting for transfers between devices: 106 us -> none  [shards(): whole = lax.all_gather(hidden, TENSOR, axis=3, tiled=True)]
    pallas_call x0 -> x1, Pallas kernels: none -> 87.9 us  [shards(): pl.pallas_call(functools.partial(kernel, (ring, members, groups, batch, s...]
    all_gather x2 -> x0, blocking collectives: 38.4 us -> none  [gathered_once(): both, at, found = (lax.all_gather(jnp.concatenate(lines), axis), 0, {})]
    all_to_all x1 -> x0, starting transfers between devices: 17.4 us -> none  [from_everyone(): lax.all_to_all(jnp.broadcast_to(x[None], (peers, *x.shape)), axis, 0, 0,...]
    all_gather x1 -> x0, local copies, waits for them, and re-layouts: 11.8 us -> none  [shards(): whole = lax.all_gather(hidden, TENSOR, axis=3, tiled=True)]
    dot_general x1 -> x0, matrix products: 7.38 us -> none  [shards(): logits = jnp.dot(normed, weight, preferred_element_type=jnp.float32)]
    reduce_sum x4 -> x0, other arithmetic: 6.84 us -> none  [the longest x1 4.24 us: shards(): mean_sq = jnp.mean(flat * flat, axis=1, keepdims=True)]
    squeeze x64 -> x0, local copies, waits for them, and re-layouts: 4.56 us -> none  [the longest x56 3.99 us: joined_all(): x = combine(x, jax.tree.map(lambda part: part[k], pieces))]
  transfers between devices with their start and end apart: 2 -> 0, of which waited for: 2 -> 0; matrix products, arithmetic and copies ran while one was open for 1% -> 0% of each run, Pallas kernels for 0% -> 0%
where the time goes in v1:
time: 92.4 us; the launch traced here: 92.2 us
  Pallas kernels  87.9 us (95%)
  local copies, waits for them, and re-layouts  3.61 us (4%)
    pallas_call x1, Pallas kernels, shards(): pl.pallas_call(functools.partial(kernel, (ring, members, groups, batch, s...  87.9 us
    unnamed x3, local copies, waits for them, and re-layouts  3.61 us

profile of v1, /device:TPU:1, one launch (start us, length us, event | category | flops | bytes accessed | tf_op | source)
XLA Modules:
  0.0 92.2 jit_solution(8798279325960498240)
XLA Ops:
  0.6 87.9 %shard_map.76 = (f32[16,96]{1,0:T(8,128)}, f32[1,16]{1,0:T(1,128)}, f32[1,16]{1,0:T(1,128)}) custom-call(bf16[16,32,96]{2,1,0:T(8,128)(2,1)} %bitcast.8, f32[1,2048]{1,0:T(1,128)} %gain_hbm.1, bf16[2048,1024]{1,0:T(8,128)(2,1)} %bitcast.7, s32[16,96]{1,0:T(8,128)} %target_hbm.1, s32[16]{0:T(128)} %length_ref.1), custom_call_target="tpu_custom_call" | custom-call | tf_op jit(solution)/shard_map/pallas_call | solution.py:393
  88.6 1.3 %copy.11 = f32[1,16,96]{2,1,0:T(8,128)} copy(f32[1,16,96]{2,1,0:T(8,128)} %bitcast.9) | data formatting | bytes 12288
  89.9 1.1 %copy.12 = f32[16]{0:T(128)} copy(f32[16]{0:T(128)} %bitcast.11) | data formatting | bytes 128
  91.0 1.2 %copy.13 = f32[16]{0:T(128)} copy(f32[16]{0:T(128)} %bitcast.10) | data formatting | bytes 128

commit v2 on v0

v2 whole, which is shorter than its diff:
```python
import functools

import jax
import jax.numpy as jnp
from jax import lax
from jax.experimental import pallas as pl
from jax.experimental.pallas import tpu as pltpu
from jax.sharding import Mesh
from jax.sharding import PartitionSpec as P

MESH = pl.DeviceIdType.MESH
TENSOR = ("tensor_0", "tensor_1")
LANES = 128
RMS_EPSILON = 1e-05
RING = 8
FIRST, SECOND, THIRD, FOURTH, FIFTH, PREPARE, UNIT = range(7)
OWNED = 3

GROUPS = ((0, 1), (1, 2), (3, 3))
ORDER = (
    (0, 0, 1), (0, 1, 1), (5, 0, 0), (0, 2, 1), (5, 1, 0), (1, 0, 0), (1, 1, 0), (5, 2, 0),
    (1, 2, 0), (5, 3, 0), (0, 0, 2), (1, 0, -1), (1, 0, 1), (0, 1, 2), (1, 1, -1), (1, 1, 1),
    (0, 2, 2), (2, 0, 0), (1, 2, -1), (1, 2, 1), (0, 0, 3), (1, 0, -2), (1, 0, 2), (2, 0, -1),
    (0, 1, 3), (1, 1, -2), (1, 1, 2), (2, 0, 1), (0, 2, 3), (1, 2, -2), (1, 2, 2), (0, 0, 4),
    (1, 0, -3), (1, 0, 3), (2, 0, -2), (0, 1, 4), (1, 1, -3), (1, 1, 3), (2, 0, 2), (2, 1, -1),
    (0, 2, 4), (1, 2, -3), (1, 2, 3), (1, 0, 4), (2, 0, -3), (2, 0, 3), (1, 1, 4), (2, 1, -2),
    (2, 1, -3), (2, 1, 0), (2, 1, 1), (1, 2, 4), (2, 1, 2), (2, 1, 3), (2, 0, 4), (2, 2, -1),
    (2, 1, 4), (2, 2, -2), (2, 2, -3), (2, 2, 0), (2, 2, 1), (2, 2, 2), (3, 0, 0), (2, 2, 3),
    (2, 2, 4), (3, 1, 0), (3, 2, 0), (4, 0, 0), (3, 3, 0), (4, 1, 0), (3, 4, 0), (6, 0, 0),
    (4, 2, 0), (6, 0, 1), (3, 5, 0), (6, 0, 2), (6, 1, 0), (4, 3, 0), (6, 1, 1), (4, 4, 0),
    (6, 1, 2), (6, 2, 0), (6, 2, 1), (4, 5, 0), (6, 2, 2), (6, 3, 0), (6, 3, 1), (6, 3, 2),
    (6, 4, 0), (6, 4, 1), (6, 4, 2), (6, 5, 0), (6, 5, 1), (6, 5, 2),
)

def kernel(
    sizes,
    hidden_hbm,
    gain_hbm,
    weight_hbm,
    target_hbm,
    length_hbm,
    token_hbm,
    ensemble_hbm,
    centered_hbm,
    gathered,
    hidden_own,
    gain_own,
    weight_own,
    target_own,
    length_own,
    weight_turned,
    gain_wide,
    target_lanes,
    logits,
    normed,
    part,
    owned_y,
    owned_z,
    owned_score,
    stats_y,
    stats_z,
    scores,
    examples,
    token_out,
    ensemble_out,
    centered_out,
    load_sem,
    send_sem,
    recv_sem,
    stat_sem,
    end_sem,
):
    ring, members, groups, batch, seq, width = sizes
    chunks = gathered.shape[0]
    units = chunks // 2
    depth = ring * ring * width
    vocab = weight_own.shape[1]
    s, d = lax.axis_index("seed"), lax.axis_index("dp")
    z, y = lax.axis_index("tensor_0"), lax.axis_index("tensor_1")

    def along_z(k):
        return lax.rem(z + (k + ring), ring)

    def along_y(k):
        return lax.rem(y + (k + ring), ring)

    loads = [
        pltpu.make_async_copy(hidden_hbm, hidden_own, load_sem.at[0]),
        pltpu.make_async_copy(target_hbm, target_own, load_sem.at[1]),
        pltpu.make_async_copy(gain_hbm, gain_own, load_sem.at[2]),
        pltpu.make_async_copy(length_hbm, length_own, load_sem.at[3]),
        pltpu.make_async_copy(weight_hbm, weight_own, load_sem.at[4]),
    ]
    loads[0].start()
    barrier = pltpu.get_barrier_semaphore()
    others = [(a, b) for a in range(members) for b in range(groups) if a or b]
    for k in (1, -1):
        pl.semaphore_signal(barrier, inc=1, device_id={"tensor_0": along_z(k)}, device_id_type=MESH)
        pl.semaphore_signal(barrier, inc=1, device_id={"tensor_1": along_y(k)}, device_id_type=MESH)
    for a, b in others:
        pl.semaphore_signal(
            barrier,
            inc=1,
            device_id={"seed": lax.rem(s + a, members), "dp": lax.rem(d + b, groups)},
            device_id_type=MESH,
        )
    for load in loads[1:]:
        load.start()

    loads[0].wait()
    for q in range(batch // 4):
        joined = lanes_joined([hidden_own[4 * q + r].astype(jnp.float32) for r in range(4)])
        for r in range(3):
            gathered[3 * q + r, z, y] = joined[r].astype(jnp.bfloat16)
    pl.semaphore_wait(barrier, 4 + len(others))

    sides = [(kind, sign) for kind in (0, 1) for sign in (1, -1)]

    arrival = {}

    def send(key, view, at, axis, sign):
        what, g, k = key
        if key not in arrival:
            arrival[key] = len(arrival)
        pltpu.make_async_remote_copy(
            src_ref=view(*at),
            dst_ref=view(*at),
            send_sem=send_sem.at[5 if (what, k) == (FIRST, 4) else what],
            recv_sem=recv_sem.at[arrival[key]],
            device_id={"tensor_0": along_z(sign)} if axis == 0 else {"tensor_1": along_y(sign)},
            device_id_type=MESH,
        ).start()

    def bulk(ref, which, number):
        return pltpu.make_async_remote_copy(
            src_ref=ref,
            dst_ref=ref,
            send_sem=send_sem.at[which],
            recv_sem=recv_sem.at[number],
            device_id={"tensor_0": along_z(1)},
            device_id_type=MESH,
        )

    waited = set()

    def need(what, g, k):
        if (what, g, k) in waited:
            return
        waited.add((what, g, k))
        if what in (FIRST, SECOND):
            ref = gathered.at[pl.ds(0, GROUPS[g][1]), 0, pl.ds(0, 2 if (what, k) == (FIRST, 4) else 4)]
        elif what == THIRD:
            ref = gathered.at[pl.ds(0, GROUPS[g][1]), pl.ds(0, 4)]
        else:
            ref = gathered.at[0, pl.ds(0, 4 if what == FOURTH else 2)]
        bulk(ref, what, arrival[what, g, k]).wait_recv()

    def wait_sends():
        refs = (
            gathered.at[:, 0, pl.ds(0, 6)],
            gathered.at[:, pl.ds(0, 2)],
            gathered.at[:, pl.ds(0, 2)],
            gathered.at[:, pl.ds(0, 2)],
            gathered.at[:, 0],
            gathered.at[:, 0, pl.ds(0, 1)],
        )
        for which, ref in enumerate(refs):
            bulk(ref, which, 0).wait_send()

    def place(kind, first, second):
        return (second, first) if kind == 0 else (first, second)

    def shards_at(kind, g, piece):
        begin, number = GROUPS[g]

        def view(dz, dy):
            return gathered.at[
                pl.ds(kind * units + begin, number), along_z(dz), along_y(dy), pl.ds(*piece)
            ]

        return view

    def block_at(kind, c, piece):
        def view(dz, dy):
            if kind == 0:
                return gathered.at[c, along_z(dz), pl.ds(*piece)]
            return gathered.at[units + c, pl.ds(*piece), along_y(dy)]

        return view

    group_of = {
        c: g for g, (begin, number) in enumerate(GROUPS) for c in range(begin, begin + number)
    }

    def transfer(what, g, k):
        if what == FIRST:
            if k > 1:
                need(FIRST, g, k - 1)
        elif what == SECOND:
            if k:
                need(FIRST, g, abs(k))
        elif what == THIRD:
            need(SECOND, g, k)
        elif what == FOURTH:
            need(THIRD, group_of[g], 0)
        else:
            need(FOURTH, g, 0)
        for kind, sign in sides:
            first_axis = 1 if kind == 0 else 0
            if what == FIRST:
                piece = (0, width) if k < 4 else ((0, width // 2), (width // 2, width // 2))[sign < 0]
                at, axis = place(kind, -(k - 1) * sign, 0), first_axis
                view = shards_at(kind, g, piece)
            elif what in (SECOND, THIRD):
                at, axis = place(kind, k, 0 if what == SECOND else -sign), 1 - first_axis
                view = shards_at(kind, g, (0, width))
            elif what == FOURTH:
                at, axis = place(kind, 0, -2 * sign), 1 - first_axis
                view = block_at(kind, g, (0, ring))
            else:
                at, axis = place(kind, 0, -3 * sign), 1 - first_axis
                view = block_at(kind, g, ((0, ring // 2), (ring // 2, ring // 2))[sign < 0])
            send((what, g, 0 if what == THIRD else k), view, at, axis, sign)

    steps = 4

    def prepare(k):
        if k == 0:
            for load in loads[1:]:
                load.wait()
            for q in range(batch // 4):
                joined = lanes_joined([target_own[pl.ds(4 * q + r, 1), :] for r in range(4)])
                for r in range(3):
                    target_lanes[pl.ds(3 * q + r, 1), :] = joined[r]
            for b in range(depth // LANES):
                row = gain_own[:, b * LANES : (b + 1) * LANES]
                gain_wide[b * LANES : (b + 1) * LANES, :] = jnp.broadcast_to(row, (LANES, LANES)).T
            for j in range(2 * OWNED, ring):
                part[j] = jnp.ones(part.shape[1:], jnp.float32)
        for b in range(k * depth // 256 // steps, (k + 1) * depth // 256 // steps):
            for v in range(vocab // 256):
                block = weight_own[b * 256 : (b + 1) * 256, v * 256 : (v + 1) * 256]
                weight_turned[v * 256 : (v + 1) * 256, b * 256 : (b + 1) * 256] = block.T

    def normalize(u):
        for side, c in enumerate((u, units + u)):
            total = jnp.zeros((1, LANES), jnp.float32)
            for b in range(depth // 256):
                x = gathered[c, b].reshape(256, LANES).astype(jnp.float32)
                total += jnp.sum(x * x, axis=0, keepdims=True)
            scale = lax.rsqrt(total * (1.0 / depth) + RMS_EPSILON)
            for b in range(depth // 256):
                x = gathered[c, b].reshape(256, LANES).astype(jnp.float32)
                gain = gain_wide[b * 256 : (b + 1) * 256, :]
                normed[b * 256 : (b + 1) * 256, side * LANES : (side + 1) * LANES] = (
                    x * scale * gain
                ).astype(jnp.bfloat16)

    def multiply(u):
        own_first = (z * ring + y) * vocab
        row = lax.broadcasted_iota(jnp.int32, (256, 2 * LANES), 0)
        wanted = jnp.concatenate(
            [target_lanes[pl.ds(c, 1), :] for c in (u, units + u)], axis=1
        )
        tiles = vocab // 256
        found = []

        def dot(v):
            logits[v * 256 : (v + 1) * 256, :] = jnp.dot(
                weight_turned[v * 256 : (v + 1) * 256, :],
                normed[...],
                preferred_element_type=jnp.float32,
            )

        def stats(v):
            block = logits[v * 256 : (v + 1) * 256, :]
            top = jnp.max(block, axis=0, keepdims=True)
            scaled = jnp.exp(block - top)
            hit = row == wanted - (own_first + v * 256)
            other = jnp.where(hit, 0.0, scaled)
            found.append(
                (
                    top,
                    jnp.sum(other, axis=0, keepdims=True),
                    jnp.sum(other * other, axis=0, keepdims=True),
                    jnp.sum(jnp.where(hit, scaled, 0.0), axis=0, keepdims=True),
                )
            )

        dot(0)
        for v in range(1, tiles):
            dot(v)
            stats(v - 1)
        stats(tiles - 1)
        top = functools.reduce(jnp.maximum, [f[0] for f in found])
        scale = [jnp.exp(f[0] - top) for f in found]
        value = (
            top,
            sum(f[1] * e for f, e in zip(found, scale)),
            sum(f[2] * e * e for f, e in zip(found, scale)),
            sum(f[3] * e for f, e in zip(found, scale)),
        )
        return [[x[:, side * LANES : (side + 1) * LANES] for x in value] for side in range(2)]

    def merged(parts, wide):
        tops = parts[:, :wide]
        top = jnp.max(tops, axis=0)
        scale = jnp.exp(tops - top[None])
        return (
            top,
            jnp.sum(parts[:, wide : 2 * wide] * scale, axis=0),
            jnp.sum(parts[:, 2 * wide : 3 * wide] * scale * scale, axis=0),
            jnp.sum(parts[:, 3 * wide : 4 * wide] * scale, axis=0),
        )

    def score_of(value):
        top, other, square, wanted = value
        return jnp.sqrt(other * other + square) / (other + wanted)

    near = sorted(range(1, ring), key=lambda k: -min(k, ring - k))

    def exchange(level, slot, source, target):
        mine = y if level == 0 else z

        def copy(src, dst, k):
            return pltpu.make_async_remote_copy(
                src_ref=src,
                dst_ref=dst,
                send_sem=stat_sem.at[0, slot],
                recv_sem=stat_sem.at[1, slot],
                device_id={"tensor_1": along_y(k)} if level == 0 else {"tensor_0": along_z(k)},
                device_id_type=MESH,
            )

        for k in near:
            copy(source(k), target(mine), k).start()
        seven = part.at[pl.ds(0, ring - 1)]
        return copy(seven, seven, 1)

    def share(u, level, value):
        buffer = stats_y if level == 0 else stats_z
        i = u - OWNED
        buffer[i, y if level == 0 else z] = jnp.concatenate(value, axis=0)
        mine = y if level == 0 else z
        return exchange(
            level, 2 * i + level, lambda k: buffer.at[i, mine], lambda p: buffer.at[i, p]
        )

    def tile(value):
        rows = jnp.concatenate(value, axis=0)
        return jnp.concatenate([rows, jnp.zeros((8 - rows.shape[0], LANES), jnp.float32)], axis=0)

    base = 2 * (units - OWNED)
    back = {}

    def after(u, rows):
        if u < OWNED:
            part[u] = tile(rows[0])
            part[OWNED + u] = tile(rows[1])
            if u == OWNED - 1:
                owned_y[y] = part[y]
                back["owned", 0] = exchange(
                    0, base, lambda k: part.at[along_y(k)], lambda p: owned_y.at[p]
                )
            return
        value = [jnp.concatenate([rows[0][k], rows[1][k]], axis=0) for k in range(4)]
        back[u, 0] = share(u, 0, value)
        if u == units - 2:
            back["owned", 0].wait_recv()
            owned_z[z] = tile(merged(owned_y[...], 1))
            back["owned", 1] = exchange(
                1, base + 1, lambda k: owned_z.at[z], lambda p: owned_z.at[p]
            )

    def second_level(u):
        back[u, 0].wait_recv()
        back[u, 1] = share(u, 1, merged(stats_y[u - OWNED], 2))

    def finish(u):
        back[u, 1].wait_recv()
        score = score_of(merged(stats_z[u - OWNED], 2))
        scores[pl.ds(u, 1), :] = score[0:1]
        scores[pl.ds(units + u, 1), :] = score[1:2]

    for what, g, k in ORDER:
        if what == PREPARE:
            prepare(g)
        elif what == UNIT:
            if k == 0:
                need(FIFTH, g, 0)
                normalize(g)
            elif k == 1:
                after(g, multiply(g))
        else:
            transfer(what, g, k)
    for u in range(OWNED, units - 1):
        second_level(u)
    back["owned", 1].wait_recv()
    owned_score[y] = jnp.broadcast_to(score_of(merged(owned_z[...], 1)), (8, LANES))
    back["owned", 2] = exchange(
        0, base + 2, lambda k: owned_score.at[y], lambda p: owned_score.at[p]
    )
    second_level(units - 1)
    example = lax.broadcasted_iota(jnp.int32, (batch, seq), 0)
    length = jnp.zeros((batch, seq), jnp.int32)
    for b in range(batch):
        length = jnp.where(example == b, length_own[b], length)
    valid = lax.broadcasted_iota(jnp.int32, (batch, seq), 1) < length
    wait_sends()
    for u in range(OWNED, units - 1):
        finish(u)
    back["owned", 2].wait_recv()
    for u in range(OWNED):
        scores[pl.ds(u, 1), :] = owned_score[u, 0:1, :]
        scores[pl.ds(units + u, 1), :] = owned_score[OWNED + u, 0:1, :]
    finish(units - 1)

    for q in range(batch // 4):
        row = [scores[pl.ds(3 * q + r, 1), :] for r in range(3)]
        split = [
            row[0][:, :seq],
            jnp.concatenate([row[0][:, 96:], row[1][:, :64]], axis=1),
            jnp.concatenate([row[1][:, 64:], row[2][:, :32]], axis=1),
            row[2][:, 32:],
        ]
        for r in range(4):
            token_out[pl.ds(4 * q + r, 1), :] = split[r]
    token = jnp.where(valid, token_out[...], 0.0)
    token_out[...] = token
    mean = jnp.sum(token, axis=1, keepdims=True) / length.astype(jnp.float32)[:, :1]
    examples[s * groups + d] = jnp.broadcast_to(mean, (batch, LANES))

    def end_copy(src, dst, a, b):
        return pltpu.make_async_remote_copy(
            src_ref=src,
            dst_ref=dst,
            send_sem=end_sem.at[0],
            recv_sem=end_sem.at[1],
            device_id={"seed": lax.rem(s + a, members), "dp": lax.rem(d + b, groups)},
            device_id_type=MESH,
        )

    own_place = s * groups + d
    for a, b in others:
        end_copy(examples.at[own_place], examples.at[own_place], a, b).start()
    rest = examples.at[pl.ds(0, len(others))]
    stores = [pltpu.make_async_copy(token_out, token_hbm, load_sem.at[5])]
    stores[0].start()
    end_copy(rest, rest, *others[0]).wait_recv()
    total = jnp.zeros((batch, LANES), jnp.float32)
    own = jnp.zeros((batch, LANES), jnp.float32)
    for b in range(groups):
        pair = examples[b]
        for a in range(1, members):
            pair += examples[a * groups + b]
        pair = pair * (1.0 / members)
        total += pair
        own = jnp.where(d == b, pair, own)
    average = jnp.sum(total, axis=0, keepdims=True) * (1.0 / (groups * batch))
    row = lax.broadcasted_iota(jnp.int32, (batch, LANES), 0)
    lane = lax.broadcasted_iota(jnp.int32, (batch, LANES), 1)
    ensemble = jnp.sum(jnp.where(row == lane, own, 0.0), axis=0, keepdims=True)
    ensemble_out[...] = ensemble[:, :batch]
    centered_out[...] = (ensemble - average)[:, :batch]
    stores.append(pltpu.make_async_copy(ensemble_out, ensemble_hbm, load_sem.at[6]))
    stores.append(pltpu.make_async_copy(centered_out, centered_hbm, load_sem.at[7]))
    for store in stores[1:]:
        store.start()
    end_copy(rest, rest, *others[0]).wait_send()
    for copy in back.values():
        copy.wait_send()
    for store in stores:
        store.wait()


def lanes_joined(part):
    return (
        jnp.concatenate([part[0], part[1][:, :32]], axis=1),
        jnp.concatenate([part[1][:, 32:], part[2][:, :64]], axis=1),
        jnp.concatenate([part[2][:, 64:], part[3]], axis=1),
    )


def hand_over(*refs):
    count = len(refs) // 2
    copies = [
        pltpu.make_async_copy(refs[k], refs[count + k], refs[-1].at[k]) for k in range(count)
    ]
    for copy in copies:
        copy.start()
    for copy in copies:
        copy.wait()


def shards(members, groups, hidden, norm_gain, lm_head, targets, lengths):
    batch, seq, width = hidden.shape[1:]
    depth, vocab = lm_head.shape[1:]
    chunks = batch * seq // LANES
    units = chunks // 2
    direct = units - OWNED
    far = pl.BlockSpec(memory_space=pl.ANY)
    f32 = jnp.float32
    outs = (
        jax.ShapeDtypeStruct((batch, seq), f32),
        jax.ShapeDtypeStruct((1, batch), f32),
        jax.ShapeDtypeStruct((1, batch), f32),
    )
    result = pl.pallas_call(
        functools.partial(kernel, (RING, members, groups, batch, seq, width)),
        out_shape=outs,
        in_specs=[far] * 5,
        out_specs=(far, far, far),
        scratch_shapes=[
            pltpu.VMEM((chunks, RING, RING, width, LANES), jnp.bfloat16),
            pltpu.VMEM((batch, width, seq), jnp.bfloat16),
            pltpu.VMEM((1, depth), f32),
            pltpu.VMEM((depth, vocab), jnp.bfloat16),
            pltpu.VMEM((batch, seq), jnp.int32),
            pltpu.SMEM((batch,), jnp.int32),
            pltpu.VMEM((vocab, depth), jnp.bfloat16),
            pltpu.VMEM((depth, LANES), f32),
            pltpu.VMEM((chunks, LANES), jnp.int32),
            pltpu.VMEM((vocab, 2 * LANES), f32),
            pltpu.VMEM((depth, 2 * LANES), jnp.bfloat16),
            pltpu.VMEM((RING, 8, LANES), f32),
            pltpu.VMEM((RING, 8, LANES), f32),
            pltpu.VMEM((RING, 8, LANES), f32),
            pltpu.VMEM((RING, 8, LANES), f32),
            pltpu.VMEM((direct, RING, 8, LANES), f32),
            pltpu.VMEM((direct, RING, 8, LANES), f32),
            pltpu.VMEM((chunks, LANES), f32),
            pltpu.VMEM((members * groups, batch, LANES), f32),
            pltpu.VMEM((batch, seq), f32),
            pltpu.VMEM((1, batch), f32),
            pltpu.VMEM((1, batch), f32),
            pltpu.SemaphoreType.DMA((8,)),
            pltpu.SemaphoreType.DMA((6,)),
            pltpu.SemaphoreType.DMA((13 * len(GROUPS) + 2 * units,)),
            pltpu.SemaphoreType.DMA((2, 2 * direct + 3)),
            pltpu.SemaphoreType.DMA((2,)),
        ],
        compiler_params=pltpu.CompilerParams(
            collective_id=0, has_side_effects=True, vmem_limit_bytes=67043328
        ),
    )(
        hidden[0].transpose(0, 2, 1),
        norm_gain,
        lm_head[0],
        targets,
        lengths,
    )
    token, ensemble, centered = pl.pallas_call(
        hand_over,
        out_shape=outs,
        in_specs=[far] * 3,
        out_specs=(far, far, far),
        scratch_shapes=[pltpu.SemaphoreType.DMA((3,))],
    )(*result)
    return token[None], ensemble[0], centered[0]


def solution(mesh):
    finer = Mesh(
        mesh.devices.reshape(mesh.shape["seed"], mesh.shape["dp"], RING, RING),
        ("seed", "dp", "tensor_0", "tensor_1"),
    )
    in_specs = (
        P("seed", "dp", None, TENSOR),
        P("seed", None),
        P("seed", None, TENSOR),
        P("dp", None),
        P("dp"),
    )
    out_specs = (P("seed", "dp", None), P("dp"), P("dp"))
    return jax.shard_map(
        functools.partial(shards, mesh.shape["seed"], mesh.shape["dp"]),
        mesh=finer,
        in_specs=in_specs,
        out_specs=out_specs,
        check_vma=False,
    )
```

time: 220 us -> 73.3 us (0.33)
  waiting for transfers between devices: 110 us -> 0 us
  Pallas kernels: 0 us -> 72.4 us
  blocking collectives: 38.4 us -> 0 us
  local copies, waits for them, and re-layouts: 20.9 us -> 0 us
  starting transfers between devices: 17.4 us -> 0 us
  between operations: 14.9 us -> 0.8 us
  other arithmetic: 10.9 us -> 0 us
  matrix products: 7.38 us -> 0 us
    all_gather x1 -> x0, waiting for transfers between devices: 106 us -> none  [shards(): whole = lax.all_gather(hidden, TENSOR, axis=3, tiled=True)]
    pallas_call x0 -> x2, Pallas kernels: none -> 72.4 us  [the longest x1 71 us: shards(): pl.pallas_call(functools.partial(kernel, (RING, members, groups, batch, s...]
    all_gather x2 -> x0, blocking collectives: 38.4 us -> none  [gathered_once(): both, at, found = (lax.all_gather(jnp.concatenate(lines), axis), 0, {})]
    all_to_all x1 -> x0, starting transfers between devices: 17.4 us -> none  [from_everyone(): lax.all_to_all(jnp.broadcast_to(x[None], (peers, *x.shape)), axis, 0, 0,...]
    all_gather x1 -> x0, local copies, waits for them, and re-layouts: 11.8 us -> none  [shards(): whole = lax.all_gather(hidden, TENSOR, axis=3, tiled=True)]
    dot_general x1 -> x0, matrix products: 7.38 us -> none  [shards(): logits = jnp.dot(normed, weight, preferred_element_type=jnp.float32)]
    reduce_sum x4 -> x0, other arithmetic: 6.84 us -> none  [the longest x1 4.24 us: shards(): mean_sq = jnp.mean(flat * flat, axis=1, keepdims=True)]
    squeeze x64 -> x0, local copies, waits for them, and re-layouts: 4.56 us -> none  [the longest x56 3.99 us: joined_all(): x = combine(x, jax.tree.map(lambda part: part[k], pieces))]
  transfers between devices with their start and end apart: 2 -> 0, of which waited for: 2 -> 0; matrix products, arithmetic and copies ran while one was open for 1% -> 0% of each run, Pallas kernels for 0% -> 0%
where the time goes in v2:
time: 73.3 us; the launch traced here: 73.2 us
  Pallas kernels  72.4 us (99%)
  between operations  0.8 us (1%)
    pallas_call x1, Pallas kernels, shards(): pl.pallas_call(functools.partial(kernel, (RING, members, groups, batch, s...  71 us

profile of v2, /device:TPU:1, one launch (start us, length us, event | category | flops | bytes accessed | tf_op | source)
XLA Modules:
  0.0 73.2 jit_solution(1697348226683904528)
XLA Ops:
  0.6 71.0 %shard_map.76 = (f32[16,96]{1,0:T(8,128)}, f32[1,16]{1,0:T(1,128)}, f32[1,16]{1,0:T(1,128)}) custom-call(bf16[16,32,96]{2,1,0:T(8,128)(2,1)} %bitcast.8, f32[1,2048]{1,0:T(1,128)} %gain_hbm.1, bf16[2048,1024]{1,0:T(8,128)(2,1)} %bitcast.7, s32[16,96]{1,0:T(8,128)} %target_hbm.1, s32[16]{0:T(128)} %length_hbm.1), custom_call_target="tpu_custom_call" | custom-call | tf_op jit(solution)/shard_map/pallas_call | solution.py:508
  71.6 1.4 %shard_map.77 = (f32[16,96]{1,0:T(8,128)}, f32[1,16]{1,0:T(1,128)}, f32[1,16]{1,0:T(1,128)}) custom-call(f32[16,96]{1,0:T(8,128)} %get-tuple-element.9.refs_0_, f32[1,16]{1,0:T(1,128)} %get-tuple-element.10.refs_1_, f32[1,16]{1,0:T(1,128)} %get-tuple-element.11.refs_2_), custom_call_target="tpu_custom_call" | custom-call | tf_op jit(solution)/shard_map/pallas_call | solution.py:552

commit v3 on v2

--- a/solution.py
+++ b/solution.py
@@ -14,22 +14,19 @@
 RMS_EPSILON = 1e-05
 RING = 8
 FIRST, SECOND, THIRD, FOURTH, FIFTH, PREPARE, UNIT = range(7)
-OWNED = 3
-
-GROUPS = ((0, 1), (1, 2), (3, 3))
+OWNED = 2
+
+GROUPS = ((0, 2), (2, 4))
 ORDER = (
-    (0, 0, 1), (0, 1, 1), (5, 0, 0), (0, 2, 1), (5, 1, 0), (1, 0, 0), (1, 1, 0), (5, 2, 0),
-    (1, 2, 0), (5, 3, 0), (0, 0, 2), (1, 0, -1), (1, 0, 1), (0, 1, 2), (1, 1, -1), (1, 1, 1),
-    (0, 2, 2), (2, 0, 0), (1, 2, -1), (1, 2, 1), (0, 0, 3), (1, 0, -2), (1, 0, 2), (2, 0, -1),
-    (0, 1, 3), (1, 1, -2), (1, 1, 2), (2, 0, 1), (0, 2, 3), (1, 2, -2), (1, 2, 2), (0, 0, 4),
-    (1, 0, -3), (1, 0, 3), (2, 0, -2), (0, 1, 4), (1, 1, -3), (1, 1, 3), (2, 0, 2), (2, 1, -1),
-    (0, 2, 4), (1, 2, -3), (1, 2, 3), (1, 0, 4), (2, 0, -3), (2, 0, 3), (1, 1, 4), (2, 1, -2),
-    (2, 1, -3), (2, 1, 0), (2, 1, 1), (1, 2, 4), (2, 1, 2), (2, 1, 3), (2, 0, 4), (2, 2, -1),
-    (2, 1, 4), (2, 2, -2), (2, 2, -3), (2, 2, 0), (2, 2, 1), (2, 2, 2), (3, 0, 0), (2, 2, 3),
-    (2, 2, 4), (3, 1, 0), (3, 2, 0), (4, 0, 0), (3, 3, 0), (4, 1, 0), (3, 4, 0), (6, 0, 0),
-    (4, 2, 0), (6, 0, 1), (3, 5, 0), (6, 0, 2), (6, 1, 0), (4, 3, 0), (6, 1, 1), (4, 4, 0),
-    (6, 1, 2), (6, 2, 0), (6, 2, 1), (4, 5, 0), (6, 2, 2), (6, 3, 0), (6, 3, 1), (6, 3, 2),
-    (6, 4, 0), (6, 4, 1), (6, 4, 2), (6, 5, 0), (6, 5, 1), (6, 5, 2),
+    (0, 0, 1), (0, 1, 1), (5, 0, 0), (1, 1, 0), (5, 1, 0), (5, 2, 0), (1, 0, 0), (5, 3, 0),
+    (0, 0, 2), (1, 0, -1), (1, 0, 1), (0, 1, 2), (1, 1, -1), (2, 0, 0), (2, 1, 0), (0, 0, 3),
+    (2, 0, -1), (2, 0, 1), (1, 0, -2), (0, 1, 3), (1, 1, 2), (1, 1, -2), (0, 0, 4), (1, 0, 3),
+    (1, 0, -3), (1, 0, 2), (2, 0, -2), (2, 1, -1), (0, 1, 4), (1, 1, 3), (1, 0, 4), (2, 0, 3),
+    (2, 0, -3), (2, 0, 2), (1, 1, -3), (2, 1, 2), (1, 1, 4), (2, 0, 4), (2, 1, 3), (1, 1, 1),
+    (2, 1, -3), (2, 1, -2), (2, 1, 4), (3, 0, 0), (2, 1, 1), (3, 1, 0), (4, 0, 0), (3, 2, 0),
+    (3, 3, 0), (4, 1, 0), (6, 0, 0), (3, 4, 0), (6, 0, 1), (4, 2, 0), (3, 5, 0), (6, 1, 0),
+    (4, 3, 0), (6, 1, 1), (4, 4, 0), (6, 2, 0), (6, 2, 1), (4, 5, 0), (6, 3, 0), (6, 3, 1),
+    (6, 4, 0), (6, 4, 1), (6, 5, 0), (6, 5, 1),
 )
 
 def kernel(
@@ -69,6 +66,7 @@
     recv_sem,
     stat_sem,
     end_sem,
+    hello,
 ):
     ring, members, groups, batch, seq, width = sizes
     chunks = gathered.shape[0]
@@ -97,13 +95,14 @@
     for k in (1, -1):
         pl.semaphore_signal(barrier, inc=1, device_id={"tensor_0": along_z(k)}, device_id_type=MESH)
         pl.semaphore_signal(barrier, inc=1, device_id={"tensor_1": along_y(k)}, device_id_type=MESH)
-    for a, b in others:
-        pl.semaphore_signal(
-            barrier,
-            inc=1,
-            device_id={"seed": lax.rem(s + a, members), "dp": lax.rem(d + b, groups)},
-            device_id_type=MESH,
-        )
+
+
+    def peer(a, b):
+        return {"seed": lax.rem(s + a, members), "dp": lax.rem(d + b, groups)}
+
+    beside = [(1, 0), (0, 1), (0, groups - 1)]
+    for a, b in beside:
+        pl.semaphore_signal(barrier, inc=1, device_id=peer(a, b), device_id_type=MESH)
     for load in loads[1:]:
         load.start()
 
@@ -112,7 +111,7 @@
         joined = lanes_joined([hidden_own[4 * q + r].astype(jnp.float32) for r in range(4)])
         for r in range(3):
             gathered[3 * q + r, z, y] = joined[r].astype(jnp.bfloat16)
-    pl.semaphore_wait(barrier, 4 + len(others))
+    pl.semaphore_wait(barrier, 4 + len(beside))
 
     sides = [(kind, sign) for kind in (0, 1) for sign in (1, -1)]
 
@@ -226,6 +225,8 @@
 
     def prepare(k):
         if k == 0:
+            for a, b in beside:
+                pl.semaphore_signal(hello.at[0], inc=1, device_id=peer(a, b), device_id_type=MESH)
             for load in loads[1:]:
                 load.wait()
             for q in range(batch // 4):
@@ -242,12 +243,19 @@
                 block = weight_own[b * 256 : (b + 1) * 256, v * 256 : (v + 1) * 256]
                 weight_turned[v * 256 : (v + 1) * 256, b * 256 : (b + 1) * 256] = block.T
 
+    def square_sum(u, side, ks):
+        total = jnp.zeros((8, LANES), jnp.float32)
+        for k in ks:
+            x = gathered[u, along_z(k)] if side == 0 else gathered[units + u, :, along_y(k)]
+            x = x.astype(jnp.float32).reshape(ring * width // 8, 8, LANES)
+            total += jnp.sum(x * x, axis=0)
+        return total
+
     def normalize(u):
+        early = [square_sum(u, side, range(-3, 4)) for side in range(2)]
+        need(FIFTH, u, 0)
         for side, c in enumerate((u, units + u)):
-            total = jnp.zeros((1, LANES), jnp.float32)
-            for b in range(depth // 256):
-                x = gathered[c, b].reshape(256, LANES).astype(jnp.float32)
-                total += jnp.sum(x * x, axis=0, keepdims=True)
+            total = jnp.sum(early[side] + square_sum(u, side, (4,)), axis=0, keepdims=True)
             scale = lax.rsqrt(total * (1.0 / depth) + RMS_EPSILON)
             for b in range(depth // 256):
                 x = gathered[c, b].reshape(256, LANES).astype(jnp.float32)
@@ -256,51 +264,61 @@
                     x * scale * gain
                 ).astype(jnp.bfloat16)
 
+    tiles = vocab // 256
+    own_first = (z * ring + y) * vocab
+    row = lax.broadcasted_iota(jnp.int32, (256, 2 * LANES), 0).reshape(32, 8, 2 * LANES)
+    found = {}
+
+    def dot(v):
+        logits[v * 256 : (v + 1) * 256, :] = jnp.dot(
+            weight_turned[v * 256 : (v + 1) * 256, :],
+            normed[...],
+            preferred_element_type=jnp.float32,
+        )
+
+    def stats(u, v):
+        wanted = jnp.concatenate([target_lanes[pl.ds(c, 1), :] for c in (u, units + u)], axis=1)
+        block = logits[v * 256 : (v + 1) * 256, :].reshape(32, 8, 2 * LANES)
+        top = jnp.max(block, axis=0)
+        scaled = jnp.exp(block - top[None])
+        hit = row == (wanted - (own_first + v * 256))[None]
+        other = jnp.where(hit, 0.0, scaled)
+        found.setdefault(u, []).append(
+            (
+                top,
+                jnp.sum(other, axis=0),
+                jnp.sum(other * other, axis=0),
+                jnp.sum(jnp.where(hit, scaled, 0.0), axis=0),
+            )
+        )
+
+    def joined(u):
+        top = functools.reduce(jnp.maximum, [f[0] for f in found[u]])
+        top = jnp.max(top, axis=0, keepdims=True)
+        scale = [jnp.exp(f[0] - top) for f in found[u]]
+        value = [
+            sum(f[1] * e for f, e in zip(found[u], scale)),
+            sum(f[2] * (e * e) for f, e in zip(found[u], scale)),
+            sum(f[3] * e for f, e in zip(found[u], scale)),
+        ]
+        value = [top] + [jnp.sum(x, axis=0, keepdims=True) for x in value]
+        return [[x[:, side * LANES : (side + 1) * LANES] for x in value] for side in range(2)]
+
     def multiply(u):
-        own_first = (z * ring + y) * vocab
-        row = lax.broadcasted_iota(jnp.int32, (256, 2 * LANES), 0)
-        wanted = jnp.concatenate(
-            [target_lanes[pl.ds(c, 1), :] for c in (u, units + u)], axis=1
-        )
-        tiles = vocab // 256
-        found = []
-
-        def dot(v):
-            logits[v * 256 : (v + 1) * 256, :] = jnp.dot(
-                weight_turned[v * 256 : (v + 1) * 256, :],
-                normed[...],
-                preferred_element_type=jnp.float32,
-            )
-
-        def stats(v):
-            block = logits[v * 256 : (v + 1) * 256, :]
-            top = jnp.max(block, axis=0, keepdims=True)
-            scaled = jnp.exp(block - top)
-            hit = row == wanted - (own_first + v * 256)
-            other = jnp.where(hit, 0.0, scaled)
-            found.append(
-                (
-                    top,
-                    jnp.sum(other, axis=0, keepdims=True),
-                    jnp.sum(other * other, axis=0, keepdims=True),
-                    jnp.sum(jnp.where(hit, scaled, 0.0), axis=0, keepdims=True),
-                )
-            )
-
         dot(0)
+        late = 0 < u < units - 1
+        if late:
+            stats(u - 1, tiles - 1)
+            before = joined(u - 1)
         for v in range(1, tiles):
             dot(v)
-            stats(v - 1)
-        stats(tiles - 1)
-        top = functools.reduce(jnp.maximum, [f[0] for f in found])
-        scale = [jnp.exp(f[0] - top) for f in found]
-        value = (
-            top,
-            sum(f[1] * e for f, e in zip(found, scale)),
-            sum(f[2] * e * e for f, e in zip(found, scale)),
-            sum(f[3] * e for f, e in zip(found, scale)),
-        )
-        return [[x[:, side * LANES : (side + 1) * LANES] for x in value] for side in range(2)]
+            stats(u, v - 1)
+        if u >= units - 2:
+            stats(u, tiles - 1)
+            own = joined(u)
+            after(u, own)
+        if late:
+            after(u - 1, before)
 
     def merged(parts, wide):
         tops = parts[:, :wide]
@@ -365,12 +383,6 @@
             return
         value = [jnp.concatenate([rows[0][k], rows[1][k]], axis=0) for k in range(4)]
         back[u, 0] = share(u, 0, value)
-        if u == units - 2:
-            back["owned", 0].wait_recv()
-            owned_z[z] = tile(merged(owned_y[...], 1))
-            back["owned", 1] = exchange(
-                1, base + 1, lambda k: owned_z.at[z], lambda p: owned_z.at[p]
-            )
 
     def second_level(u):
         back[u, 0].wait_recv()
@@ -387,20 +399,24 @@
             prepare(g)
         elif what == UNIT:
             if k == 0:
-                need(FIFTH, g, 0)
+                if g == 0:
+                    pl.semaphore_wait(hello.at[0], len(beside))
+                    pl.semaphore_signal(hello.at[1], inc=1, device_id=peer(1, 0), device_id_type=MESH)
                 normalize(g)
             elif k == 1:
-                after(g, multiply(g))
+                multiply(g)
         else:
             transfer(what, g, k)
-    for u in range(OWNED, units - 1):
+    back["owned", 0].wait_recv()
+    owned_z[z] = tile(merged(owned_y[...], 1))
+    back["owned", 1] = exchange(1, base + 1, lambda k: owned_z.at[z], lambda p: owned_z.at[p])
+    for u in range(OWNED, units):
         second_level(u)
     back["owned", 1].wait_recv()
     owned_score[y] = jnp.broadcast_to(score_of(merged(owned_z[...], 1)), (8, LANES))
     back["owned", 2] = exchange(
         0, base + 2, lambda k: owned_score.at[y], lambda p: owned_score.at[p]
     )
-    second_level(units - 1)
     example = lax.broadcasted_iota(jnp.int32, (batch, seq), 0)
     length = jnp.zeros((batch, seq), jnp.int32)
     for b in range(batch):
@@ -436,10 +452,11 @@
             dst_ref=dst,
             send_sem=end_sem.at[0],
             recv_sem=end_sem.at[1],
-            device_id={"seed": lax.rem(s + a, members), "dp": lax.rem(d + b, groups)},
+            device_id=peer(a, b),
             device_id_type=MESH,
         )
 
+    pl.semaphore_wait(hello.at[1], 1)
     own_place = s * groups + d
     for a, b in others:
         end_copy(examples.at[own_place], examples.at[own_place], a, b).start()
@@ -538,6 +555,7 @@
             pltpu.SemaphoreType.DMA((13 * len(GROUPS) + 2 * units,)),
             pltpu.SemaphoreType.DMA((2, 2 * direct + 3)),
             pltpu.SemaphoreType.DMA((2,)),
+            pltpu.SemaphoreType.REGULAR((2,)),
         ],
         compiler_params=pltpu.CompilerParams(
             collective_id=0, has_side_effects=True, vmem_limit_bytes=67043328

time: 73.3 us -> 72.7 us (level)
  no operation moved by 1% of the time
where the time goes in v3:
time: 72.7 us; the launch traced here: 72.6 us
  Pallas kernels  71.9 us (99%)
    pallas_call x1, Pallas kernels, shards(): pl.pallas_call(functools.partial(kernel, (RING, members, groups, batch, s...  70.5 us

profile of v3, /device:TPU:1, one launch (start us, length us, event | category | flops | bytes accessed | tf_op | source)
XLA Modules:
  0.0 72.6 jit_solution(6488841849776812710)
XLA Ops:
  0.6 70.5 %shard_map.76 = (f32[16,96]{1,0:T(8,128)}, f32[1,16]{1,0:T(1,128)}, f32[1,16]{1,0:T(1,128)}) custom-call(bf16[16,32,96]{2,1,0:T(8,128)(2,1)} %bitcast.8, f32[1,2048]{1,0:T(1,128)} %gain_hbm.1, bf16[2048,1024]{1,0:T(8,128)(2,1)} %bitcast.7, s32[16,96]{1,0:T(8,128)} %target_hbm.1, s32[16]{0:T(128)} %length_hbm.1), custom_call_target="tpu_custom_call" | custom-call | tf_op jit(solution)/shard_map/pallas_call | solution.py:525
  71.2 1.4 %shard_map.77 = (f32[16,96]{1,0:T(8,128)}, f32[1,16]{1,0:T(1,128)}, f32[1,16]{1,0:T(1,128)}) custom-call(f32[16,96]{1,0:T(8,128)} %get-tuple-element.9.refs_0_, f32[1,16]{1,0:T(1,128)} %get-tuple-element.10.refs_1_, f32[1,16]{1,0:T(1,128)} %get-tuple-element.11.refs_2_), custom_call_target="tpu_custom_call" | custom-call | tf_op jit(solution)/shard_map/pallas_call | solution.py:570

commit v4 on v3

--- a/solution.py
+++ b/solution.py
@@ -444,7 +444,12 @@
     token = jnp.where(valid, token_out[...], 0.0)
     token_out[...] = token
     mean = jnp.sum(token, axis=1, keepdims=True) / length.astype(jnp.float32)[:, :1]
-    examples[s * groups + d] = jnp.broadcast_to(mean, (batch, LANES))
+    diagonal = lax.broadcasted_iota(jnp.int32, (batch, LANES), 0) == lax.broadcasted_iota(
+        jnp.int32, (batch, LANES), 1
+    )
+    examples[s * groups + d] = jnp.sum(
+        jnp.where(diagonal, jnp.broadcast_to(mean, (batch, LANES)), 0.0), axis=0, keepdims=True
+    )
 
     def end_copy(src, dst, a, b):
         return pltpu.make_async_remote_copy(
@@ -464,19 +469,16 @@
     stores = [pltpu.make_async_copy(token_out, token_hbm, load_sem.at[5])]
     stores[0].start()
     end_copy(rest, rest, *others[0]).wait_recv()
-    total = jnp.zeros((batch, LANES), jnp.float32)
-    own = jnp.zeros((batch, LANES), jnp.float32)
+    total = jnp.zeros((1, LANES), jnp.float32)
+    ensemble = jnp.zeros((1, LANES), jnp.float32)
     for b in range(groups):
         pair = examples[b]
         for a in range(1, members):
             pair += examples[a * groups + b]
         pair = pair * (1.0 / members)
         total += pair
-        own = jnp.where(d == b, pair, own)
-    average = jnp.sum(total, axis=0, keepdims=True) * (1.0 / (groups * batch))
-    row = lax.broadcasted_iota(jnp.int32, (batch, LANES), 0)
-    lane = lax.broadcasted_iota(jnp.int32, (batch, LANES), 1)
-    ensemble = jnp.sum(jnp.where(row == lane, own, 0.0), axis=0, keepdims=True)
+        ensemble = jnp.where(d == b, pair, ensemble)
+    average = jnp.sum(total, axis=1, keepdims=True) * (1.0 / (groups * batch))
     ensemble_out[...] = ensemble[:, :batch]
     centered_out[...] = (ensemble - average)[:, :batch]
     stores.append(pltpu.make_async_copy(ensemble_out, ensemble_hbm, load_sem.at[6]))
@@ -546,7 +548,7 @@
             pltpu.VMEM((direct, RING, 8, LANES), f32),
             pltpu.VMEM((direct, RING, 8, LANES), f32),
             pltpu.VMEM((chunks, LANES), f32),
-            pltpu.VMEM((members * groups, batch, LANES), f32),
+            pltpu.VMEM((members * groups, 1, LANES), f32),
             pltpu.VMEM((batch, seq), f32),
             pltpu.VMEM((1, batch), f32),
             pltpu.VMEM((1, batch), f32),

time: 72.7 us -> 72.3 us (level)
  no operation moved by 1% of the time
where the time goes in v4:
time: 72.3 us; the launch traced here: 72.1 us
  Pallas kernels  71.5 us (99%)
    pallas_call x1, Pallas kernels, shards(): pl.pallas_call(functools.partial(kernel, (RING, members, groups, batch, s...  70.1 us

profile of v4, /device:TPU:1, one launch (start us, length us, event | category | flops | bytes accessed | tf_op | source)
XLA Modules:
  0.0 72.1 jit_solution(10593461579797699899)
XLA Ops:
  0.6 70.1 %shard_map.76 = (f32[16,96]{1,0:T(8,128)}, f32[1,16]{1,0:T(1,128)}, f32[1,16]{1,0:T(1,128)}) custom-call(bf16[16,32,96]{2,1,0:T(8,128)(2,1)} %bitcast.8, f32[1,2048]{1,0:T(1,128)} %gain_hbm.1, bf16[2048,1024]{1,0:T(8,128)(2,1)} %bitcast.7, s32[16,96]{1,0:T(8,128)} %target_hbm.1, s32[16]{0:T(128)} %length_hbm.1), custom_call_target="tpu_custom_call" | custom-call | tf_op jit(solution)/shard_map/pallas_call | solution.py:527
  70.7 1.4 %shard_map.77 = (f32[16,96]{1,0:T(8,128)}, f32[1,16]{1,0:T(1,128)}, f32[1,16]{1,0:T(1,128)}) custom-call(f32[16,96]{1,0:T(8,128)} %get-tuple-element.9.refs_0_, f32[1,16]{1,0:T(1,128)} %get-tuple-element.10.refs_1_, f32[1,16]{1,0:T(1,128)} %get-tuple-element.11.refs_2_), custom_call_target="tpu_custom_call" | custom-call | tf_op jit(solution)/shard_map/pallas_call | solution.py:572
